TPU v7x, 256 devices: a whole 4x4x8 slice. The times are simulated.
256 devices in a mesh: grp: 32 (over y, x, core), rest: 8 (over z).
Axes of the slice: x: 4, y: 4, z: 8, core: 2. Of those that a mesh axis runs over, the one named last changes fastest.
Arguments:
- grads: bfloat16 [32, 18432, 1024], P('grp', 'rest'), parts along dimension 1, may hold values from -6 to 6
- weight: bfloat16 [18432, 1024], P('rest'), parts along dimension 0, may hold values from -0.625 to 0.625
- moment1: float32 [2304, 8192], P('grp', 'rest'), parts along dimension 1, may hold values from -2 to 2
- moment2: float32 [2304, 8192], P('grp', 'rest'), parts along dimension 1, may hold values from 0.0001 to 0.04
- step: int32 [1], replicated, may hold values from 1 to 8
Outputs:
- new_weight: bfloat16 [18432, 1024], P('rest'), parts along dimension 0
- new_moment1: float32 [2304, 8192], P('grp', 'rest'), parts along dimension 1
- new_moment2: float32 [2304, 8192], P('grp', 'rest'), parts along dimension 1
There are 8 independent parts, one for each index of `rest`. A program takes and returns all parts, laid end to end along the dimension named above; an argument that names none is the same for every part. Nothing has to cross between parts.
All inputs are finite; a program needn't handle non-finite values.
Results may differ from a plain program's by a relative error of at most 0.006.
Values may be sent and summed in bfloat16 or wider, within the bound.
A program may use at most 128 MiB of HBM per device.

v0:
```python
import jax
import jax.numpy as jnp
from jax import lax
from jax.sharding import PartitionSpec as P


def split_up(shard, dim, devices):
    before, after = (shard.shape[:dim], shard.shape[dim + 1 :])
    return jnp.moveaxis(shard.reshape(*before, devices, -1, *after), dim, 0)


def cut_rows(length, count):
    lap = length // count
    if lap >= 8:
        lap -= lap % 8
    return [lap * k for k in range(1, count)]


def joined_along(pieces, dim):
    pieces = jnp.moveaxis(pieces, 0, dim)
    dims = pieces.shape
    return pieces.reshape(*dims[:dim], dims[dim] * dims[dim + 1], *dims[dim + 2 :])


def exchange_in_pieces(shard, axis, pieces, split_dim, concat_dim):
    blocks = split_up(shard, split_dim, lax.axis_size(axis))
    widest = max(range(1, max(2, blocks.ndim - 1)), key=lambda d: blocks.shape[d])
    done = []
    for piece in jnp.split(blocks, cut_rows(blocks.shape[widest], pieces), axis=widest):
        if piece.size:
            done.append(lax.all_to_all(piece, axis, split_axis=0, concat_axis=0, tiled=True))
    return joined_along(jnp.concatenate(done, axis=widest), concat_dim)


def adamw_rows(summed, moment1, moment2, owned_rows, step_count, groups):
    average = summed / groups
    new_moment1 = 0.9 * moment1 + 0.1 * average
    new_moment2 = 0.999 * moment2 + 0.001 * average * average
    first_hat = new_moment1 / (1.0 - jnp.power(jnp.float32(0.9), step_count))
    second_hat = new_moment2 / (1.0 - jnp.power(jnp.float32(0.999), step_count))
    updated = owned_rows.astype(jnp.float32) * (1.0 - 0.25 * 0.1) - 0.25 * first_hat / (
        jnp.sqrt(second_hat) + 1e-08
    )
    return (updated.astype(jnp.bfloat16), new_moment1, new_moment2)


def shards(grads, weight, moment1, moment2, step):
    groups = lax.axis_size("grp")
    row_count = moment1.shape[0]
    first_row = lax.axis_index("grp") * row_count
    owned_rows = lax.dynamic_slice_in_dim(weight, first_row, row_count, 0)
    step_count = step[0].astype(jnp.float32)
    tile_stack = exchange_in_pieces(grads, "grp", 2, 1, 0)
    summed = jnp.sum(tile_stack, axis=0, dtype=jnp.float32)
    updated, first_part, second_part = adamw_rows(
        summed, moment1, moment2, owned_rows, step_count, groups
    )
    pieces_weight = lax.all_gather(updated, "grp", axis=0, tiled=True)
    return (pieces_weight, first_part, second_part)


def solution(mesh):
    return jax.shard_map(
        shards,
        mesh=mesh,
        in_specs=(P("grp", "rest", None), P("rest", None), P("grp", "rest"), P("grp", "rest"), P()),
        out_specs=(P("rest", None), P("grp", "rest"), P("grp", "rest")),
        check_vma=False,
    )
```

profile of v0, /device:TPU:1, one launch (start us, length us, event | category | flops | bytes accessed | tf_op | source)
XLA Modules:
  0.0 157.2 jit_solution(15604907398098677836)
XLA Ops:
  7.2 3.2 %split.8 = bf16[32,1,32,1024]{3,2,1,0:T(8,128)(2,1)} slice(bf16[32,1,72,1024]{3,2,1,0:T(8,128)(2,1)} %bitcast.3), slice={[0:32], [0:1], [0:32], [0:1024]} | slice | bytes 4194304 | tf_op jit(solution)/shard_map/split | solution.py:29
  10.4 8.6 %all-to-all-start = ((bf16[32,1,32,1024]{3,2,1,0:T(8,128)(2,1)}), bf16[32,1,32,1024]{3,2,1,0:T(8,128)(2,1)S(1)}, u32[]{:S(2)}, u32[]{:S(2)}) async-start(bf16[32,1,32,1024]{3,2,1,0:T(8,128)(2,1)} %split.8), calls=%async_computation | async-start | bytes 4194304 | tf_op jit(solution)/shard_map/all_to_all | solution.py:31
  19.0 3.5 %split.9 = bf16[32,1,40,1024]{3,2,1,0:T(8,128)(2,1)} slice(bf16[32,1,72,1024]{3,2,1,0:T(8,128)(2,1)} %bitcast.4), slice={[0:32], [0:1], [32:72], [0:1024]} | slice | bytes 5242880 | tf_op jit(solution)/shard_map/split | solution.py:29
  22.5 0.0 copy-start.1
  22.5 0.0 copy-start.2
  22.5 25.1 %all-to-all-done = bf16[32,1,32,1024]{3,2,1,0:T(8,128)(2,1)S(1)} async-done(((bf16[32,1,32,1024]{3,2,1,0:T(8,128)(2,1)}), bf16[32,1,32,1024]{3,2,1,0:T(8,128)(2,1)S(1)}, u32[]{:S(2)}, u32[]{:S(2)}) %all-to-all-start) | async-done | bytes 2097184 | tf_op jit(solution)/shard_map/all_to_all | solution.py:31
  47.6 0.0 copy-start
  47.6 1.3 copy-done
  48.9 5.4 %all-to-all-start.1 = ((bf16[32,1,40,1024]{3,2,1,0:T(8,128)(2,1)}), bf16[32,1,40,1024]{3,2,1,0:T(8,128)(2,1)S(1)}, u32[]{:S(2)}, u32[]{:S(2)}) async-start(bf16[32,1,40,1024]{3,2,1,0:T(8,128)(2,1)} %split.9), calls=%async_computation.1 | async-start | bytes 5242880 | tf_op jit(solution)/shard_map/all_to_all | solution.py:31
  54.3 0.0 all-gather.2.cloned.1.call-start
  55.1 33.2 %all-to-all-done.1 = bf16[32,1,40,1024]{3,2,1,0:T(8,128)(2,1)S(1)} async-done(((bf16[32,1,40,1024]{3,2,1,0:T(8,128)(2,1)}), bf16[32,1,40,1024]{3,2,1,0:T(8,128)(2,1)S(1)}, u32[]{:S(2)}, u32[]{:S(2)}) %all-to-all-start.1) | async-done | bytes 2621472 | tf_op jit(solution)/shard_map/all_to_all | solution.py:31
  88.3 2.7 %convert_reduce_fusion = f32[72,1024]{1,0:T(8,128)S(1)} fusion(bf16[32,1,40,1024]{3,2,1,0:T(8,128)(2,1)S(1)} %all-to-all-done.1, bf16[32,1,32,1024]{3,2,1,0:T(8,128)(2,1)} %copy-done), kind=kLoop, calls=%fused_computation | loop fusion | flops 11722752 | bytes 5013504 | tf_op jit(solution)/shard_map/reduce_sum | solution.py:54
  91.1 0.0 copy-done.1
  91.1 0.0 copy-done.2
  91.1 1.9 %subtract_convert_fusion = (bf16[72,1024]{1,0:T(8,128)(2,1)}, f32[72,1024]{1,0:T(8,128)}, f32[72,1024]{1,0:T(8,128)}) fusion(f32[]{:T(128)} %bitcast.2, f32[]{:T(128)} %bitcast.1, bf16[2304,1024]{1,0:T(8,128)(2,1)} %param.6, s32[]{:T(128)S(6)} %select_n.3, f32[72,1024]{1,0:T(8,128)S(1)} %convert_reduce_fusion, f32[72,1024]{1,0:T(8,128)S(1)} %copy-done.1, ...), kind=kLoop, calls=%fused_computation.1 | loop fusion | flops 1253376 | bytes 1769484 | tf_op jit(solution)/shard_map/convert_element_type | solution.py:44
  93.0 0.0 all-gather.2.cloned.1.call-update
  93.0 52.3 %all-gather.2.cloned.1.call-done = bf16[2304,1024]{1,0:T(8,128)(2,1)} async-done(((bf16[72,1024]{1,0:T(8,128)(2,1)}), bf16[2304,1024]{1,0:T(8,128)(2,1)}) %all-gather.2.cloned.1.call-update) | async-done | bytes 4718608 | tf_op jit(solution)/shard_map/all_gather | solution.py:58
  145.3 5.0 %copy.10 = bf16[2304,1024]{1,0:T(8,128)(2,1)} copy(bf16[2304,1024]{1,0:T(8,128)(2,1)} %all-gather.2.cloned.1.call-done) | data formatting | bytes 9437184
Async XLA Ops:
  10.4 37.2 %all-to-all-start = ((bf16[32,1,32,1024]{3,2,1,0:T(8,128)(2,1)}), bf16[32,1,32,1024]{3,2,1,0:T(8,128)(2,1)S(1)}, u32[]{:S(2)}, u32[]{:S(2)}) async-start(bf16[32,1,32,1024]{3,2,1,0:T(8,128)(2,1)} %split.8), calls=%async_computation | async-start | bytes 4194304 | tf_op jit(solution)/shard_map/all_to_all | solution.py:31
  22.5 68.6 %copy-start.1 = (f32[72,1024]{1,0:T(8,128)S(1)}, f32[72,1024]{1,0:T(8,128)}, u32[]{:S(2)}) copy-start(f32[72,1024]{1,0:T(8,128)} %param.7) | copy-start | bytes 884740
  22.5 68.6 %copy-start.2 = (f32[72,1024]{1,0:T(8,128)S(1)}, f32[72,1024]{1,0:T(8,128)}, u32[]{:S(2)}) copy-start(f32[72,1024]{1,0:T(8,128)} %param.8) | copy-start | bytes 884740
  47.6 1.3 copy-start
  48.9 39.4 %all-to-all-start.1 = ((bf16[32,1,40,1024]{3,2,1,0:T(8,128)(2,1)}), bf16[32,1,40,1024]{3,2,1,0:T(8,128)(2,1)S(1)}, u32[]{:S(2)}, u32[]{:S(2)}) async-start(bf16[32,1,40,1024]{3,2,1,0:T(8,128)(2,1)} %split.9), calls=%async_computation.1 | async-start | bytes 5242880 | tf_op jit(solution)/shard_map/all_to_all | solution.py:31
  54.3 91.0 %all-gather.2.cloned.1.call-start = ((), (), s32[]{:S(2)}) async-start(), calls=%async_computation.2 | async-start | bytes 4866048 | tf_op jit(solution)/shard_map/all_gather | solution.py:58
Sparse Core Ops, SparseCore 0:
  93.1 52.1 all-gather.1
where the time goes:
time: 158 us; the launch traced here: 157 us
  waiting for transfers between devices  111 us (70%)
  between operations  14.8 us (9%)
  starting transfers between devices  14 us (9%)
  local copies, waits for them, and re-layouts  13.1 us (8%)
  other arithmetic  4.66 us (3%)
    all_to_all x2, waiting for transfers between devices, exchange_in_pieces(): lax.all_to_all(piece, axis, split_axis=0, concat_axis=0, tiled=True)  58.3 us
    all_gather x1, waiting for transfers between devices, shards(): pieces_weight = lax.all_gather(updated, 'grp', axis=0, tiled=True)  52.3 us
    all_to_all x2, starting transfers between devices, exchange_in_pieces(): lax.all_to_all(piece, axis, split_axis=0, concat_axis=0, tiled=True)  14 us
    split x2, local copies, waits for them, and re-layouts, exchange_in_pieces(): jnp.split(blocks, cut_rows(blocks.shape[widest], pieces), axis=widest)  6.71 us
    unnamed x7, local copies, waits for them, and re-layouts  6.38 us
  transfers between devices with their start and end apart: 3, of which 3 were waited for; matrix products, arithmetic and copies ran while one was open for 2% of the time, Pallas kernels for 0%

commit v1 on v0

v1 whole, which is shorter than its diff:
```python
import functools

import jax
import jax.numpy as jnp
import numpy as np
from jax import lax
from jax.experimental import pallas as pl
from jax.experimental.pallas import tpu as pltpu
from jax.sharding import PartitionSpec as P

SIDE = 4
CORES = 2
LANES = 128
PIECES = (192, 192, 192)

OFFSETS = (0, 1, 3, 2)
PLUS, MINUS = 0, 1


def sem_keys(pieces):
    keys = []
    for p in range(pieces):
        keys += [("D", p, j) for j in range(4)]
        keys += [(k, p, h) for k in ("A", "S", "B", "A2", "S2", "B2") for h in range(2)]
        keys += [(k, p, d) for k in ("GB", "FB") for d in range(2)]
        keys += [(k, p, d, q) for k in ("GA", "FA") for d in range(2) for q in range(4)]
        keys += [("P", p, da, q) for da in range(4) for q in range(4)]
    return {k: i for i, k in enumerate(keys)}


def powers(base, steps):
    base = float(np.float32(base))
    out = jnp.ones(steps.shape, jnp.float32)
    for k in range(31):
        out = jnp.where(((steps >> k) & 1) == 1, out * np.float32(base ** (2**k)), out)
    return out


def exchange_kernel(
    sizes, ids,
    step_ref, g_ref, w_ref, m1_ref, m2_ref,
    out, nm1, nm2,
    raw, rx, ra, rs, rb, ra2, rs2, rb2, wv, m1v, m2v,
    send_sems, recv_sems, load_sems,
):
    pieces = len(sizes)
    starts = [sum(sizes[:p]) for p in range(pieces)]
    g = lax.axis_index("grp")
    y, x, c = g // (SIDE * CORES), (g // CORES) % SIDE, g % CORES
    a = x * (1 - c) + y * c
    b = y * (1 - c) + x * c

    def at(da, db):
        ny = (y + da * c + db * (1 - c)) % SIDE
        nx = (x + da * (1 - c) + db * c) % SIDE
        return {"grp": (ny * SIDE + nx) * CORES + c}

    to_a = (at(1, 0), at(3, 0))
    to_b = (at(0, 1), at(0, 3))
    partner = {"grp": g + 1 - 2 * c}
    a_at = [(a + d) % SIDE for d in range(SIDE)]
    b_at = [(b + d) % SIDE for d in range(SIDE)]

    barrier = pltpu.get_barrier_semaphore()
    for device in (partner, *to_a, *to_b):
        pl.semaphore_signal(barrier, inc=1, device_id=device, device_id_type=pl.DeviceIdType.MESH)

    def rows(p, half=None):
        if half is None:
            return pl.ds(starts[p], sizes[p])
        return pl.ds(starts[p] + half * (sizes[p] // 2), sizes[p] // 2)

    def hrows(p):
        return pl.ds(starts[p] // 2, sizes[p] // 2)

    loads = []

    def load(src, dst):
        copy = pltpu.make_async_copy(src, dst, load_sems.at[len(loads)])
        copy.start()
        loads.append(copy)
        return copy

    piece_loads = []
    for p in range(pieces):
        mine = []
        for k in range(SIDE):
            mine.append(load(g_ref.at[:, k, 0, rows(p)], raw.at[0, k, :, rows(p)]))
            mine.append(load(g_ref.at[k, :, 1, rows(p)], raw.at[1, k, :, rows(p)]))
        piece_loads.append(mine)
    state_loads = [load(w_ref.at[y, x, c], wv), load(m1_ref, m1v), load(m2_ref, m2v)]

    sent = []

    def send(key, src, dst, device):
        copy = pltpu.make_async_remote_copy(
            src_ref=src, dst_ref=dst,
            send_sem=send_sems.at[ids[key]], recv_sem=recv_sems.at[ids[key]],
            device_id=device, device_id_type=pl.DeviceIdType.MESH,
        )
        copy.start()
        sent.append(copy)

    def arrived(key, dst, device):
        pltpu.make_async_remote_copy(
            src_ref=dst, dst_ref=dst,
            send_sem=send_sems.at[ids[key]], recv_sem=recv_sems.at[ids[key]],
            device_id=device, device_id_type=pl.DeviceIdType.MESH,
        ).wait_recv()

    pl.semaphore_wait(barrier, 5)

    for p in range(pieces):
        for copy in piece_loads[p]:
            copy.wait()
        for j, d in enumerate((2, 1, 3, 0)):
            send(("D", p, j), raw.at[1 - c, b_at[d], :, rows(p)], rx.at[b_at[d], :, rows(p)], partner)

    def each(body):
        def step(i, carry):
            body(i)
            return carry

        lax.fori_loop(0, SIDE, step, 0)

    def paired(p, j, d):
        arrived(("D", p, j), rx.at[a_at[d], :, rows(p)], partner)

        def body(i):
            raw[c, a_at[d], i, rows(p)] = raw[c, a_at[d], i, rows(p)] + rx[a_at[d], i, rows(p)]

        each(body)

    def f32(value):
        return value.astype(jnp.float32)

    def first_sends(p):
        paired(p, 0, 2)
        for h in range(2):
            send(("A", p, h), raw.at[c, a_at[2], :, rows(p, h)], ra.at[h, :, hrows(p)], to_a[h])
        paired(p, 1, 1)
        send(("S", p, 1), raw.at[c, a_at[1], :, rows(p, 1)], rs.at[1, :, hrows(p)], to_a[PLUS])
        paired(p, 2, 3)
        send(("S", p, 0), raw.at[c, a_at[3], :, rows(p, 0)], rs.at[0, :, hrows(p)], to_a[MINUS])
        paired(p, 3, 0)

    def first_relay(p):
        for h in range(2):
            far = a_at[1 + 2 * h]
            arrived(("A", p, h), ra.at[h, :, hrows(p)], to_a[h])

            def body(i):
                raw[c, far, i, rows(p, h)] = raw[c, far, i, rows(p, h)] + ra[h, i, hrows(p)]

            each(body)
            send(("B", p, h), raw.at[c, far, :, rows(p, h)], rb.at[h, :, hrows(p)], to_a[h])

    def second_sends(p):
        for h in range(2):
            arrived(("S", p, h), rs.at[h, :, hrows(p)], to_a[h])
        for h in range(2):
            arrived(("B", p, h), rb.at[h, :, hrows(p)], to_a[h])

            def body(i):
                total = f32(raw[c, a, i, rows(p, h)]) + f32(rs[h, i, hrows(p)]) + f32(rb[h, i, hrows(p)])
                raw[c, a, i, rows(p, h)] = total.astype(jnp.bfloat16)

            each(body)
        for h in range(2):
            send(("A2", p, h), raw.at[c, a, b_at[2], rows(p, h)], ra2.at[h, hrows(p)], to_b[h])
        send(("S2", p, 1), raw.at[c, a, b_at[1], rows(p, 1)], rs2.at[1, hrows(p)], to_b[PLUS])
        send(("S2", p, 0), raw.at[c, a, b_at[3], rows(p, 0)], rs2.at[0, hrows(p)], to_b[MINUS])

    def second_relay(p):
        for h in range(2):
            far = b_at[1 + 2 * h]
            arrived(("A2", p, h), ra2.at[h, hrows(p)], to_b[h])
            raw[c, a, far, rows(p, h)] = raw[c, a, far, rows(p, h)] + ra2[h, hrows(p)]
            send(("B2", p, h), raw.at[c, a, far, rows(p, h)], rb2.at[h, hrows(p)], to_b[h])

    steps = jnp.full((8, LANES), step_ref[0], jnp.int32)
    scale1 = (1.0 / (1.0 - powers(0.9, steps)))[0:1]
    scale2 = (1.0 / (1.0 - powers(0.999, steps)))[0:1]

    def update(p):
        if p == 0:
            for copy in state_loads:
                copy.wait()
        for h in range(2):
            arrived(("S2", p, h), rs2.at[h, hrows(p)], to_b[h])
        for h in range(2):
            arrived(("B2", p, h), rb2.at[h, hrows(p)], to_b[h])
            r = rows(p, h)
            total = f32(raw[c, a, b, r]) + f32(rs2[h, hrows(p)]) + f32(rb2[h, hrows(p)])
            average = total * (1.0 / (SIDE * SIDE * CORES))
            moment1 = 0.9 * m1v[r] + 0.1 * average
            moment2 = 0.999 * m2v[r] + 0.001 * average * average
            nm1[r] = moment1
            nm2[r] = moment2
            change = 0.25 * (moment1 * scale1) / (jnp.sqrt(moment2 * scale2) + 1e-08)
            out[c, a, b, r] = (f32(wv[r]) * (1.0 - 0.25 * 0.1) - change).astype(jnp.bfloat16)
        own = out.at[c, a, b, rows(p)]
        for d in range(2):
            send(("GB", p, d), own, own, to_b[d])
        spread(p, 0)

    def to_partner(p, da, q):
        block = out.at[c, a_at[da], b_at[OFFSETS[q]], rows(p)]
        send(("P", p, da, q), block, block, partner)

    def spread(p, q):
        block = out.at[c, a, b_at[OFFSETS[q]], rows(p)]
        for d in range(2):
            send(("GA", p, d, q), block, block, to_a[d])
        to_partner(p, 0, q)

    def second_gather(p):
        for d in range(2):
            back = b_at[3 - 2 * d]
            arrived(("GB", p, d), out.at[c, a, back, rows(p)], to_b[d])
            half = out.at[c, a, back, rows(p, d)]
            send(("FB", p, d), half, half, to_b[d])
        spread(p, 1)
        spread(p, 2)

    def second_done(p):
        for d in range(2):
            arrived(("FB", p, d), out.at[c, a, b_at[2], rows(p, d)], to_b[d])
        spread(p, 3)
        relay(p, 0)

    def relay(p, q):
        for d in range(2):
            back = 3 - 2 * d
            arrived(("GA", p, d, q), out.at[c, a_at[back], b_at[OFFSETS[q]], rows(p)], to_a[d])
            half = out.at[c, a_at[back], b_at[OFFSETS[q]], rows(p, d)]
            send(("FA", p, d, q), half, half, to_a[d])
            to_partner(p, back, q)

    def landed(p, q):
        for d in range(2):
            arrived(("FA", p, d, q), out.at[c, a_at[2], b_at[OFFSETS[q]], rows(p, d)], to_a[d])
        to_partner(p, 2, q)

    def first_gather(p):
        relay(p, 1)
        relay(p, 2)
        landed(p, 0)

    def first_tail(p):
        relay(p, 3)
        landed(p, 1)
        landed(p, 2)

    def first_done(p):
        landed(p, 3)

    stages = (
        first_sends, first_relay, second_sends, second_relay, update,
        second_gather, second_done, first_gather, first_tail, first_done,
    )
    for slot in range(len(stages) + pieces - 1):
        for p in range(pieces):
            if 0 <= slot - p < len(stages):
                stages[slot - p](p)

    for p in range(pieces):
        for da in range(4):
            for q in range(4):
                arrived(("P", p, da, q), out.at[1 - c, b_at[da], a_at[OFFSETS[q]], rows(p)], partner)
    for copy in sent:
        copy.wait_send()


def store_kernel(out, nm1, nm2, w_ref, m1_ref, m2_ref, sems):
    copies = []

    def store(src, dst):
        copy = pltpu.make_async_copy(src, dst, sems.at[len(copies)])
        copy.start()
        copies.append(copy)

    for k in range(SIDE):
        store(out.at[0, k], w_ref.at[:, k, 0])
        store(out.at[1, k], w_ref.at[k, :, 1])
    store(nm1, m1_ref)
    store(nm2, m2_ref)
    for copy in copies:
        copy.wait()


def tiled(array):
    rows, columns = array.shape
    parts = array.reshape(rows // 8, 8, columns // LANES, LANES)
    return parts.transpose(0, 2, 1, 3).reshape(rows * columns // LANES, LANES)


def untiled(array, rows, columns):
    parts = array.reshape(rows // 8, columns // LANES, 8, LANES)
    return parts.transpose(0, 2, 1, 3).reshape(rows, columns)


def shards(grads, weight, moment1, moment2, step):
    own, columns = moment1.shape
    depth = own * columns // LANES
    grid = (SIDE, SIDE, CORES, depth, LANES)
    sizes = PIECES
    ids = sem_keys(len(sizes))
    bf16 = jnp.bfloat16
    vmem = pl.BlockSpec(memory_space=pltpu.VMEM)
    hbm = pl.BlockSpec(memory_space=pltpu.HBM)
    out, nm1, nm2 = pl.pallas_call(
        functools.partial(exchange_kernel, sizes, ids),
        out_shape=(
            pltpu.VMEM((CORES, SIDE, SIDE, depth, LANES), bf16),
            pltpu.VMEM((depth, LANES), jnp.float32),
            pltpu.VMEM((depth, LANES), jnp.float32),
        ),
        in_specs=[pl.BlockSpec(memory_space=pltpu.SMEM)] + [hbm] * 4,
        out_specs=(vmem,) * 3,
        scratch_shapes=[
            pltpu.VMEM((CORES, SIDE, SIDE, depth, LANES), bf16),
            pltpu.VMEM((SIDE, SIDE, depth, LANES), bf16),
            *[pltpu.VMEM((2, SIDE, depth // 2, LANES), bf16)] * 3,
            *[pltpu.VMEM((2, depth // 2, LANES), bf16)] * 3,
            pltpu.VMEM((depth, LANES), bf16),
            *[pltpu.VMEM((depth, LANES), jnp.float32)] * 2,
            pltpu.SemaphoreType.DMA((len(ids),)),
            pltpu.SemaphoreType.DMA((len(ids),)),
            pltpu.SemaphoreType.DMA((8 * len(sizes) + 3,)),
        ],
        compiler_params=pltpu.CompilerParams(collective_id=0, has_side_effects=True, vmem_limit_bytes=40 << 20),
        name="reduce_update_gather",
    )(step, *(
        pltpu.with_memory_space_constraint(array, pltpu.HBM)
        for array in (
            tiled(grads[0]).reshape(grid), tiled(weight).reshape(grid), tiled(moment1), tiled(moment2)
        )
    ))
    new_weight, new_moment1, new_moment2 = pl.pallas_call(
        store_kernel,
        out_shape=(
            jax.ShapeDtypeStruct(grid, bf16),
            jax.ShapeDtypeStruct((depth, LANES), jnp.float32),
            jax.ShapeDtypeStruct((depth, LANES), jnp.float32),
        ),
        in_specs=[vmem] * 3,
        out_specs=(hbm,) * 3,
        scratch_shapes=[pltpu.SemaphoreType.DMA((2 * SIDE + 2,))],
        compiler_params=pltpu.CompilerParams(vmem_limit_bytes=1 << 20),
        name="store",
    )(*(pltpu.with_memory_space_constraint(array, pltpu.VMEM) for array in (out, nm1, nm2)))
    return (
        untiled(new_weight.reshape(-1, LANES), *weight.shape),
        untiled(new_moment1, own, columns),
        untiled(new_moment2, own, columns),
    )


def solution(mesh):
    return jax.shard_map(
        shards,
        mesh=mesh,
        in_specs=(P("grp", "rest", None), P("rest", None), P("grp", "rest"), P("grp", "rest"), P()),
        out_specs=(P("rest", None), P("grp", "rest"), P("grp", "rest")),
        check_vma=False,
    )
```

time: 158 us -> 56.2 us (0.36)
  waiting for transfers between devices: 111 us -> 0 us
  Pallas kernels: 0 us -> 54.9 us
  starting transfers between devices: 14 us -> 0 us
  between operations: 14.8 us -> 1.29 us
  local copies, waits for them, and re-layouts: 13.1 us -> 0 us
  other arithmetic: 4.66 us -> 0 us
    all_to_all x2 -> x0, waiting for transfers between devices: 58.3 us -> none  [exchange_in_pieces(): lax.all_to_all(piece, axis, split_axis=0, concat_axis=0, tiled=True)]
    pallas_call x0 -> x2, Pallas kernels: none -> 54.9 us  [the longest x1 52.4 us: shards(): pl.pallas_call(functools.partial(exchange_kernel, sizes, ids), out_shape=...]
    all_gather x1 -> x0, waiting for transfers between devices: 52.3 us -> none  [shards(): pieces_weight = lax.all_gather(updated, 'grp', axis=0, tiled=True)]
    all_to_all x2 -> x0, starting transfers between devices: 14 us -> none  [exchange_in_pieces(): lax.all_to_all(piece, axis, split_axis=0, concat_axis=0, tiled=True)]
    split x2 -> x0, local copies, waits for them, and re-layouts: 6.71 us -> none  [exchange_in_pieces(): jnp.split(blocks, cut_rows(blocks.shape[widest], pieces), axis=widest)]
    unnamed x7 -> x0, local copies, waits for them, and re-layouts: 6.38 us -> none
    reduce_sum x1 -> x0, other arithmetic: 2.75 us -> none  [shards(): summed = jnp.sum(tile_stack, axis=0, dtype=jnp.float32)]
    convert_element_type x1 -> x0, other arithmetic: 1.91 us -> none  [adamw_rows(): return (updated.astype(jnp.bfloat16), new_moment1, new_moment2)]
  transfers between devices with their start and end apart: 3 -> 0, of which waited for: 3 -> 0; matrix products, arithmetic and copies ran while one was open for 2% -> 0% of each run, Pallas kernels for 0% -> 0%
where the time goes in v1:
time: 56.2 us
  Pallas kernels  54.9 us (98%)
  between operations  1.29 us (2%)
    pallas_call x1, Pallas kernels, shards(): pl.pallas_call(functools.partial(exchange_kernel, sizes, ids), out_shape=...  52.4 us
    pallas_call x1, Pallas kernels, shards(): pl.pallas_call(store_kernel, out_shape=(jax.ShapeDtypeStruct(grid, bf16),...  2.44 us

profile of v1, /device:TPU:1, one launch (start us, length us, event | category | flops | bytes accessed | tf_op | source)
XLA Modules:
  0.0 56.2 jit_solution(14636535953610399396)
XLA Ops:
  1.3 52.4 %reduce_update_gather.1 = (bf16[2,4,4,576,128]{4,3,2,1,0:T(8,128)(2,1)S(1)}, f32[576,128]{1,0:T(8,128)S(1)}, f32[576,128]{1,0:T(8,128)S(1)}) custom-call(s32[1]{0:T(128)S(6)} %copy.8.step_ref, bf16[4,4,2,576,128]{4,3,2,1,0:T(8,128)(2,1)} %bitcast.35, bf16[4,4,2,576,128]{4,3,2,1,0:T(8,128)(2,1)} %bitcast.36, f32[576,128]{1,0:T(8,128)} %bitcast.37, ...), custom_call_target="tpu_custom_call" | custom-call | tf_op jit(solution)/shard_map/reduce_update_gather/pallas_call | solution.py:312
  53.7 2.4 %store.1 = (bf16[4,4,2,576,128]{4,3,2,1,0:T(8,128)(2,1)}, f32[576,128]{1,0:T(8,128)}, f32[576,128]{1,0:T(8,128)}) custom-call(bf16[2,4,4,576,128]{4,3,2,1,0:T(8,128)(2,1)S(1)} %get-tuple-element.9.out, f32[576,128]{1,0:T(8,128)S(1)} %get-tuple-element.10.nm1, f32[576,128]{1,0:T(8,128)S(1)} %get-tuple-element.11.nm2), custom_call_target="tpu_custom_call" | custom-call | tf_op jit(solution)/shard_map/store/pallas_call | solution.py:340
